TPU v7x, 32 devices: a whole 2x2x4 slice. The times are simulated.
32 devices in a mesh: seq: 8 (over z, y), dp: 4 (over x, core).
Axes of the slice: x: 2, y: 2, z: 4, core: 2. Of those that a mesh axis runs over, the one named last changes fastest.
Arguments:
- hidden: bfloat16 [4, 2048, 4608], P('dp', 'seq'), may hold values from -6 to 6
- queries: bfloat16 [4, 2048, 2048], P('dp', 'seq'), may hold values from -64 to 64
- down_weight: bfloat16 [4608, 1024], P('dp'), may hold values from -0.09375 to 0.09375
- up_weight: bfloat16 [2, 512, 1024], P(None, 'dp'), may hold values from -0.25 to 0.25
- lengths: int32 [4], P('dp'), may hold values from 512 to 2048
Outputs:
- latent_cache: bfloat16 [4, 2048, 1024], P('dp', 'seq')
- attended: bfloat16 [4, 2048, 2048], P('dp', 'seq')
All inputs are finite; a program needn't handle non-finite values.
Results may differ from a plain program's by a relative error of at most 0.012.
The roundings to bfloat16 on the way count: a program that leaves them out, or rounds other values in their place, can miss the bound.
Values may be sent and summed in bfloat16 or wider, within the bound.
A program may use at most 128 MiB of HBM per device.

v0:
```python
import jax
import jax.numpy as jnp
from jax import lax
from jax.sharding import PartitionSpec as P

HEAD = 128
WINDOW = 4096


query_scale = 144.0 ** (-0.5)
soft_cap = 50.0


def rotate(values_in, start_pos):
    batches, count, width = values_in.shape
    half_head = HEAD // 2
    places = (start_pos + jnp.arange(count, dtype=jnp.int32)).astype(jnp.float32)
    freqs = 10000.0 ** (-2.0 * jnp.arange(half_head, dtype=jnp.float32) / HEAD)
    angles = places[:, None] * freqs[None, :]
    cosine = jnp.cos(angles)[None, :, None, :]
    sine_val = jnp.sin(angles)[None, :, None, :]
    split_heads = values_in.reshape(batches, count, width // HEAD, 2, half_head)
    lower = split_heads[:, :, :, 0, :]
    upper = split_heads[:, :, :, 1, :]
    turned = jnp.stack(
        [lower * cosine - upper * sine_val, upper * cosine + lower * sine_val], axis=3
    )
    return turned.reshape(batches, count, width)


def expand(latent_rows, start_pos, uppers):
    batches, count, latent_rank = latent_rows.shape
    key_rank = latent_rank // 2
    kv_width = uppers.shape[2]
    keys_raw = jnp.dot(
        latent_rows[:, :, :key_rank].reshape(-1, key_rank),
        uppers[0],
        preferred_element_type=jnp.float32,
    )
    keys_out = rotate(keys_raw.reshape(batches, count, kv_width), start_pos).astype(jnp.bfloat16)
    values_out = jnp.dot(
        latent_rows[:, :, key_rank:].reshape(-1, key_rank),
        uppers[1],
        preferred_element_type=jnp.float32,
    )
    values_out = values_out.astype(jnp.bfloat16).reshape(batches, count, kv_width)
    return jnp.stack([keys_out, values_out])


def attend(state, pairs, start_pos, q_split, q_pos):
    numer, denom = state
    batches, count, kv_width = pairs.shape[1:]
    groups = kv_width // HEAD
    keys_grp = pairs[0].reshape(batches, count, groups, HEAD)
    values_grp = pairs[1].reshape(batches, count, groups, HEAD)
    raw = jnp.einsum("blgrd,bngd->bgrln", q_split, keys_grp, preferred_element_type=jnp.float32)
    capped = soft_cap * jnp.tanh(raw * (query_scale / soft_cap))
    key_pos = start_pos + jnp.arange(count, dtype=jnp.int32)
    allowed = (
        (key_pos[None, :] <= q_pos[:, None])
        & (key_pos[None, :] > q_pos[:, None] - WINDOW)
        & (key_pos[None, :] >= 0)
    )
    expo = jnp.where(allowed, jnp.exp(capped), 0.0)
    denom = denom + jnp.sum(expo, axis=-1)
    numer = numer + jnp.einsum(
        "bgrln,bngd->blgrd",
        expo.astype(jnp.bfloat16),
        values_grp,
        preferred_element_type=jnp.float32,
    )
    return (numer, denom)


def body(hidden, queries, down_weight, up_weight, lengths):
    seq_count, local_rows, model_dim = hidden.shape
    latent_rank = down_weight.shape[1]
    flat_hidden = hidden.reshape(seq_count * local_rows, model_dim)
    latent_sum = jnp.dot(
        flat_hidden,
        lax.all_gather(down_weight, "dp", axis=0, tiled=True),
        preferred_element_type=jnp.float32,
    )
    seq_index = lax.axis_index("seq")
    own_start = seq_index * local_rows
    q_pos = own_start + jnp.arange(local_rows, dtype=jnp.int32)
    is_live = q_pos[None, :] < lengths[:, None]
    latent = latent_sum.astype(jnp.bfloat16).reshape(seq_count, local_rows, latent_rank)
    latent = jnp.where(is_live[:, :, None], latent, jnp.zeros((), jnp.bfloat16))
    uppers = lax.all_gather(up_weight, "dp", axis=1, tiled=True)
    groups = up_weight.shape[2] // HEAD
    ratio = queries.shape[2] // (groups * HEAD)
    q_split = queries.reshape(seq_count, local_rows, groups, ratio, HEAD)
    initial = (
        jnp.zeros((seq_count, local_rows, groups, ratio, HEAD), jnp.float32),
        jnp.zeros((seq_count, groups, ratio, local_rows), jnp.float32),
    )

    def unpack(travel, start_pos):
        return expand(travel, start_pos, uppers)

    tile_rows = local_rows * max(1, 512 // local_rows)
    part = lax.all_gather(latent, "seq", axis=1, tiled=True)
    row_axis = part.ndim - 2
    count = part.shape[row_axis]
    pieces = count // tile_rows
    shaped = part.reshape(part.shape[:row_axis] + (pieces, tile_rows) + part.shape[row_axis + 1 :])
    shaped = jnp.moveaxis(shaped, row_axis, 0)

    def scan_step(inner, packed):
        offset, tile_data = packed
        tile_start = offset * tile_rows
        return (attend(inner, unpack(tile_data, tile_start), tile_start, q_split, q_pos), None)

    outcome = lax.scan(scan_step, initial, (jnp.arange(pieces, dtype=jnp.int32), shaped))
    numer, denom = outcome[0]
    result = numer / jnp.transpose(denom, (0, 3, 1, 2))[..., None]
    result = result.reshape(seq_count, local_rows, groups * ratio * HEAD)
    attended = jnp.where(is_live[:, :, None], result, 0.0).astype(jnp.bfloat16)
    return (latent, attended)


def solution(mesh):
    in_specs = (
        P("dp", "seq", None),
        P("dp", "seq", None),
        P("dp", None),
        P(None, "dp", None),
        P("dp"),
    )
    out_specs = (P("dp", "seq", None), P("dp", "seq", None))
    return jax.shard_map(body, mesh=mesh, in_specs=in_specs, out_specs=out_specs, check_vma=False)
```

profile of v0, /device:TPU:28, one launch (start us, length us, event | category | flops | bytes accessed | tf_op | source)
XLA Modules:
  0.0 265.5 jit_solution(3122235590937611120)
XLA Ops:
  8.0 2.0 copy.16
  10.7 64.0 %all-gather.5.cloned.1.call-done = bf16[4608,1024]{1,0:T(8,128)(2,1)} async-done(((bf16[1152,1024]{1,0:T(8,128)(2,1)}), bf16[4608,1024]{1,0:T(8,128)(2,1)}) %all-gather.5.cloned.1.call-update) | async-done | bytes 9437200 | tf_op jit(solution)/shard_map/all_gather | solution.py:81
  74.7 7.1 %fusion.24 = bf16[256,1024]{1,0:T(8,128)(2,1)} fusion(bf16[4608,1024]{1,0:T(8,128)(2,1)} %all-gather.5.cloned.1.call-done, bf16[1,256,4608]{2,1,0:T(8,128)(2,1)S(1)} %copy-done, pred[256]{0:T(512)(128)(4,1)S(1)} %add_compare_fusion), kind=kOutput, calls=%fused_computation.37 | convolution fusion | flops 2416443392 | bytes 12321024 | tf_op jit(solution)/shard_map/dot_general | solution.py:79
  81.8 1.5 copy.17
  83.4 1.3 copy.19
  84.7 14.4 %all-gather.7.cloned.1.call-done = bf16[2,512,1024]{1,2,0:T(8,128)(2,1)} async-done(((bf16[2,128,1024]{1,2,0:T(8,128)(2,1)}), bf16[2,512,1024]{1,2,0:T(8,128)(2,1)}) %all-gather.7.cloned.1.call-update) | async-done | bytes 2097168 | tf_op jit(solution)/shard_map/all_gather | solution.py:90
  99.1 73.1 %all-gather.9.cloned.1.call-done = bf16[2048,1024]{1,0:T(8,128)(2,1)} async-done(((bf16[256,1024]{1,0:T(8,128)(2,1)}), bf16[2048,1024]{1,0:T(8,128)(2,1)}) %all-gather.9.cloned.1.call-update) | async-done | bytes 4194320 | tf_op jit(solution)/shard_map/all_gather | solution.py:103
  172.3 81.1 %while.15 = (s32[]{:T(128)}, f32[1,256,8,2,128]{1,4,3,2,0:T(8,128)}, f32[1,8,2,256]{3,2,1,0:T(2,128)S(1)}, bf16[4,1,512,1024]{3,2,1,0:T(8,128)(2,1)}, bf16[2,512...) while((s32[]{:T(128)}, ...), condition=%wide.region_2.3_spmd.clone, body=%wide.region_0.2_spmd.clone.sunk | while | flops 2169018880 | bytes 69154824 | solution.py:115
  176.9 3.0 %convolution_convert_fusion.2 = bf16[512,1024]{1,0:T(8,128)(2,1)} fusion(bf16[2,512,1024]{1,2,0:T(8,128)(2,1)} %get-tuple-element.274, bf16[1,512,1024]{2,1,0:T(8,128)(2,1)S(1)} %dynamic-slice_bitcast_fusion.2), kind=kOutput, calls=%fused_computation.9.clone.1 | convolution fusion | flops 537395200 | bytes 2621440 | tf_op jit(solution)/shard_map/while/body/eval_jaxpr/dot_general | solution.py:41
  179.9 2.3 copy.30
  182.2 1.3 slice.69
  184.8 3.5 %fusion.44 = (f32[8,2,256]{2,1,0:T(2,128)S(1)}, f32[8,512,256,2]{2,1,3,0:T(8,128)S(1)}) fusion(pred[256,512]{0,1:T(8,128)(4,1)S(1)} %copy-done.3, bf16[512,8,128,1]{0,2,3,1:T(8,128)(2,1)S(1)} %bitcast.122, bf16[1,256,8,2,128]{4,1,3,2,0:T(8,128)(2,1)S(1)} %copy-done.6), kind=kOutput, calls=%fused_computation.2.clone.1 | convolution fusion | flops 545255424 | bytes 10633216 | tf_op jit(solution)/shard_map/while/body/eval_jaxpr/blgrd,bngd->bgrln/dot_general | solution.py:56
  188.3 2.8 %bitcast_add_fusion.4 = f32[1,256,8,2,128]{1,4,3,2,0:T(8,128)S(1)} fusion(f32[1,256,8,2,128]{1,4,3,2,0:T(8,128)S(1)} %copy-done.4, bf16[512,8,128,1]{0,2,3,1:T(8,128)(2,1)S(1)} %bitcast.121, f32[8,512,256,2]{2,1,3,0:T(8,128)S(1)} %get-tuple-element.246, pred[256,512]{0,1:T(8,128)(4,1)S(1)} %copy-done.3, pred[]{:T(512)S(6)} %compare.3), kind=kOutput, calls=%fused_computation.7.clone.1 | convolution fusion | flops 546308096 | bytes 13762561 | tf_op jit(solution)/shard_map/while/body/eval_jaxpr/bgrln,bngd->blgrd/dot_general | solution.py:66
  191.2 1.3 copy-done.5
  197.2 3.0 %convolution_convert_fusion.2 = bf16[512,1024]{1,0:T(8,128)(2,1)} fusion(bf16[2,512,1024]{1,2,0:T(8,128)(2,1)} %get-tuple-element.274, bf16[1,512,1024]{2,1,0:T(8,128)(2,1)S(1)} %dynamic-slice_bitcast_fusion.2), kind=kOutput, calls=%fused_computation.9.clone.1 | convolution fusion | flops 537395200 | bytes 2621440 | tf_op jit(solution)/shard_map/while/body/eval_jaxpr/dot_general | solution.py:41
  200.2 2.3 copy.30
  202.5 1.3 slice.69
  205.1 3.5 %fusion.44 = (f32[8,2,256]{2,1,0:T(2,128)S(1)}, f32[8,512,256,2]{2,1,3,0:T(8,128)S(1)}) fusion(pred[256,512]{0,1:T(8,128)(4,1)S(1)} %copy-done.3, bf16[512,8,128,1]{0,2,3,1:T(8,128)(2,1)S(1)} %bitcast.122, bf16[1,256,8,2,128]{4,1,3,2,0:T(8,128)(2,1)S(1)} %copy-done.6), kind=kOutput, calls=%fused_computation.2.clone.1 | convolution fusion | flops 545255424 | bytes 10633216 | tf_op jit(solution)/shard_map/while/body/eval_jaxpr/blgrd,bngd->bgrln/dot_general | solution.py:56
  208.6 2.8 %bitcast_add_fusion.4 = f32[1,256,8,2,128]{1,4,3,2,0:T(8,128)S(1)} fusion(f32[1,256,8,2,128]{1,4,3,2,0:T(8,128)S(1)} %copy-done.4, bf16[512,8,128,1]{0,2,3,1:T(8,128)(2,1)S(1)} %bitcast.121, f32[8,512,256,2]{2,1,3,0:T(8,128)S(1)} %get-tuple-element.246, pred[256,512]{0,1:T(8,128)(4,1)S(1)} %copy-done.3, pred[]{:T(512)S(6)} %compare.3), kind=kOutput, calls=%fused_computation.7.clone.1 | convolution fusion | flops 546308096 | bytes 13762561 | tf_op jit(solution)/shard_map/while/body/eval_jaxpr/bgrln,bngd->blgrd/dot_general | solution.py:66
  217.4 3.0 %convolution_convert_fusion.2 = bf16[512,1024]{1,0:T(8,128)(2,1)} fusion(bf16[2,512,1024]{1,2,0:T(8,128)(2,1)} %get-tuple-element.274, bf16[1,512,1024]{2,1,0:T(8,128)(2,1)S(1)} %dynamic-slice_bitcast_fusion.2), kind=kOutput, calls=%fused_computation.9.clone.1 | convolution fusion | flops 537395200 | bytes 2621440 | tf_op jit(solution)/shard_map/while/body/eval_jaxpr/dot_general | solution.py:41
  220.5 2.3 copy.30
  222.7 1.3 slice.69
  225.4 3.5 %fusion.44 = (f32[8,2,256]{2,1,0:T(2,128)S(1)}, f32[8,512,256,2]{2,1,3,0:T(8,128)S(1)}) fusion(pred[256,512]{0,1:T(8,128)(4,1)S(1)} %copy-done.3, bf16[512,8,128,1]{0,2,3,1:T(8,128)(2,1)S(1)} %bitcast.122, bf16[1,256,8,2,128]{4,1,3,2,0:T(8,128)(2,1)S(1)} %copy-done.6), kind=kOutput, calls=%fused_computation.2.clone.1 | convolution fusion | flops 545255424 | bytes 10633216 | tf_op jit(solution)/shard_map/while/body/eval_jaxpr/blgrd,bngd->bgrln/dot_general | solution.py:56
  228.9 2.8 %bitcast_add_fusion.4 = f32[1,256,8,2,128]{1,4,3,2,0:T(8,128)S(1)} fusion(f32[1,256,8,2,128]{1,4,3,2,0:T(8,128)S(1)} %copy-done.4, bf16[512,8,128,1]{0,2,3,1:T(8,128)(2,1)S(1)} %bitcast.121, f32[8,512,256,2]{2,1,3,0:T(8,128)S(1)} %get-tuple-element.246, pred[256,512]{0,1:T(8,128)(4,1)S(1)} %copy-done.3, pred[]{:T(512)S(6)} %compare.3), kind=kOutput, calls=%fused_computation.7.clone.1 | convolution fusion | flops 546308096 | bytes 13762561 | tf_op jit(solution)/shard_map/while/body/eval_jaxpr/bgrln,bngd->blgrd/dot_general | solution.py:66
  237.7 3.0 %convolution_convert_fusion.2 = bf16[512,1024]{1,0:T(8,128)(2,1)} fusion(bf16[2,512,1024]{1,2,0:T(8,128)(2,1)} %get-tuple-element.274, bf16[1,512,1024]{2,1,0:T(8,128)(2,1)S(1)} %dynamic-slice_bitcast_fusion.2), kind=kOutput, calls=%fused_computation.9.clone.1 | convolution fusion | flops 537395200 | bytes 2621440 | tf_op jit(solution)/shard_map/while/body/eval_jaxpr/dot_general | solution.py:41
  240.7 2.3 copy.30
  243.0 1.3 slice.69
  245.6 3.5 %fusion.44 = (f32[8,2,256]{2,1,0:T(2,128)S(1)}, f32[8,512,256,2]{2,1,3,0:T(8,128)S(1)}) fusion(pred[256,512]{0,1:T(8,128)(4,1)S(1)} %copy-done.3, bf16[512,8,128,1]{0,2,3,1:T(8,128)(2,1)S(1)} %bitcast.122, bf16[1,256,8,2,128]{4,1,3,2,0:T(8,128)(2,1)S(1)} %copy-done.6), kind=kOutput, calls=%fused_computation.2.clone.1 | convolution fusion | flops 545255424 | bytes 10633216 | tf_op jit(solution)/shard_map/while/body/eval_jaxpr/blgrd,bngd->bgrln/dot_general | solution.py:56
  249.1 2.8 %bitcast_add_fusion.4 = f32[1,256,8,2,128]{1,4,3,2,0:T(8,128)S(1)} fusion(f32[1,256,8,2,128]{1,4,3,2,0:T(8,128)S(1)} %copy-done.4, bf16[512,8,128,1]{0,2,3,1:T(8,128)(2,1)S(1)} %bitcast.121, f32[8,512,256,2]{2,1,3,0:T(8,128)S(1)} %get-tuple-element.246, pred[256,512]{0,1:T(8,128)(4,1)S(1)} %copy-done.3, pred[]{:T(512)S(6)} %compare.3), kind=kOutput, calls=%fused_computation.7.clone.1 | convolution fusion | flops 546308096 | bytes 13762561 | tf_op jit(solution)/shard_map/while/body/eval_jaxpr/bgrln,bngd->blgrd/dot_general | solution.py:66
  253.3 1.8 broadcast_divide_fusion
  255.1 1.4 copy.25
  256.6 2.4 select_convert_fusion
  (127 shorter events, 25.8 us)
Async XLA Ops:
  7.2 67.6 %copy-start = (bf16[1,256,4608]{2,1,0:T(8,128)(2,1)S(1)}, bf16[1,256,4608]{2,1,0:T(8,128)(2,1)}, u32[]{:S(2)}) copy-start(bf16[1,256,4608]{2,1,0:T(8,128)(2,1)} %param.7) | copy-start | bytes 7077892
  7.2 67.5 %all-gather.5.cloned.1.call-start = ((), (), s32[]{:S(2)}) async-start(), calls=%async_computation | async-start | bytes 11796480 | tf_op jit(solution)/shard_map/all_gather | solution.py:81
  7.9 91.2 %all-gather.7.cloned.1.call-start = ((), (), s32[]{:S(2)}) async-start(), calls=%async_computation.1 | async-start | bytes 2621440 | tf_op jit(solution)/shard_map/all_gather | solution.py:90
  10.0 162.3 %all-gather.9.cloned.1.call-start = ((), (), s32[]{:S(2)}) async-start(), calls=%async_computation.2 | async-start | bytes 4718592 | tf_op jit(solution)/shard_map/all_gather | solution.py:103
  10.7 71.1 %copy-start.7 = (pred[256]{0:T(512)(128)(4,1)}, pred[256]{0:T(512)(128)(4,1)S(1)}, u32[]{:S(2)}) copy-start(pred[256]{0:T(512)(128)(4,1)S(1)} %add_compare_fusion) | copy-start | bytes 772
  172.3 1.3 copy-start.9
  182.2 2.1 copy-start.2
  183.5 1.3 copy-start.6
  184.8 3.5 %copy-start.1 = (bf16[512,1024]{0,1:T(8,128)(2,1)S(1)}, bf16[512,1024]{0,1:T(8,128)(2,1)}, u32[]{:S(2)}) copy-start(bf16[512,1024]{0,1:T(8,128)(2,1)} %copy.30) | copy-start | bytes 3145732 | tf_op jit(solution)/shard_map/while
  184.8 3.5 %copy-start.4 = (f32[1,256,8,2,128]{1,4,3,2,0:T(8,128)S(1)}, f32[1,256,8,2,128]{1,4,3,2,0:T(8,128)}, u32[]{:S(2)}) copy-start(f32[1,256,8,2,128]{1,4,3,2,0:T(8,128)} %get-tuple-element.260) | copy-start | bytes 6291460 | tf_op jit(solution)/shard_map/while
  188.3 4.2 %copy-start.10 = (s32[4]{0:T(128)S(1)}, s32[4]{0:T(128)}, u32[]{:S(2)}) copy-start(s32[4]{0:T(128)} %copy-done.9) | copy-start | bytes 52 | tf_op jit(solution)/shard_map/while
  191.2 1.3 copy-start.5
  192.5 1.3 copy-start.9
  202.5 2.1 copy-start.2
  203.8 1.3 copy-start.6
  205.1 3.5 %copy-start.1 = (bf16[512,1024]{0,1:T(8,128)(2,1)S(1)}, bf16[512,1024]{0,1:T(8,128)(2,1)}, u32[]{:S(2)}) copy-start(bf16[512,1024]{0,1:T(8,128)(2,1)} %copy.30) | copy-start | bytes 3145732 | tf_op jit(solution)/shard_map/while
  205.1 3.5 %copy-start.4 = (f32[1,256,8,2,128]{1,4,3,2,0:T(8,128)S(1)}, f32[1,256,8,2,128]{1,4,3,2,0:T(8,128)}, u32[]{:S(2)}) copy-start(f32[1,256,8,2,128]{1,4,3,2,0:T(8,128)} %get-tuple-element.260) | copy-start | bytes 6291460 | tf_op jit(solution)/shard_map/while
  208.6 4.2 %copy-start.10 = (s32[4]{0:T(128)S(1)}, s32[4]{0:T(128)}, u32[]{:S(2)}) copy-start(s32[4]{0:T(128)} %copy-done.9) | copy-start | bytes 52 | tf_op jit(solution)/shard_map/while
  211.5 1.3 copy-start.5
  222.7 2.1 copy-start.2
  224.1 1.3 copy-start.6
  225.4 3.5 %copy-start.1 = (bf16[512,1024]{0,1:T(8,128)(2,1)S(1)}, bf16[512,1024]{0,1:T(8,128)(2,1)}, u32[]{:S(2)}) copy-start(bf16[512,1024]{0,1:T(8,128)(2,1)} %copy.30) | copy-start | bytes 3145732 | tf_op jit(solution)/shard_map/while
  225.4 3.5 %copy-start.4 = (f32[1,256,8,2,128]{1,4,3,2,0:T(8,128)S(1)}, f32[1,256,8,2,128]{1,4,3,2,0:T(8,128)}, u32[]{:S(2)}) copy-start(f32[1,256,8,2,128]{1,4,3,2,0:T(8,128)} %get-tuple-element.260) | copy-start | bytes 6291460 | tf_op jit(solution)/shard_map/while
  228.8 4.2 %copy-start.10 = (s32[4]{0:T(128)S(1)}, s32[4]{0:T(128)}, u32[]{:S(2)}) copy-start(s32[4]{0:T(128)} %copy-done.9) | copy-start | bytes 52 | tf_op jit(solution)/shard_map/while
  231.7 1.3 copy-start.5
  243.0 2.1 copy-start.2
  244.3 1.3 copy-start.6
  245.6 3.5 %copy-start.1 = (bf16[512,1024]{0,1:T(8,128)(2,1)S(1)}, bf16[512,1024]{0,1:T(8,128)(2,1)}, u32[]{:S(2)}) copy-start(bf16[512,1024]{0,1:T(8,128)(2,1)} %copy.30) | copy-start | bytes 3145732 | tf_op jit(solution)/shard_map/while
  245.6 3.5 %copy-start.4 = (f32[1,256,8,2,128]{1,4,3,2,0:T(8,128)S(1)}, f32[1,256,8,2,128]{1,4,3,2,0:T(8,128)}, u32[]{:S(2)}) copy-start(f32[1,256,8,2,128]{1,4,3,2,0:T(8,128)} %get-tuple-element.260) | copy-start | bytes 6291460 | tf_op jit(solution)/shard_map/while
  249.1 4.2 %copy-start.10 = (s32[4]{0:T(128)S(1)}, s32[4]{0:T(128)}, u32[]{:S(2)}) copy-start(s32[4]{0:T(128)} %copy-done.9) | copy-start | bytes 52 | tf_op jit(solution)/shard_map/while
  252.0 1.3 copy-start.5
  253.3 3.2 %copy-start.8 = (pred[256]{0:T(512)(128)(4,1)S(1)}, pred[256]{0:T(512)(128)(4,1)}, u32[]{:S(2)}) copy-start(pred[256]{0:T(512)(128)(4,1)} %copy-done.7) | copy-start | bytes 772
  (6 other events, 7.6 us)
Sparse Core Ops, SparseCore 0:
  9.5 65.1 all-gather.4
  76.3 22.8 all-gather.6
  101.8 70.3 all-gather.8
where the time goes:
time: 271 us; the launch traced here: 266 us
  waiting for transfers between devices  152 us (56%)
  matrix products  47.4 us (17%)
  local copies, waits for them, and re-layouts  33.7 us (12%)
  other arithmetic  14.5 us (5%)
  between operations  14.5 us (5%)
  loops' own time  3.1 us (1%)
    all_gather x1, waiting for transfers between devices, body(): part = lax.all_gather(latent, 'seq', axis=1, tiled=True)  73.1 us
    all_gather x1, waiting for transfers between devices, body(): lax.all_gather(down_weight, 'dp', axis=0, tiled=True)  64 us
    all_gather x1, waiting for transfers between devices, body(): uppers = lax.all_gather(up_weight, 'dp', axis=1, tiled=True)  14.4 us
    dot_general x4, matrix products, attend(): jnp.einsum('blgrd,bngd->bgrln', q_split, keys_grp, preferred_element_type...  13.8 us
    dot_general x4, matrix products, expand(): jnp.dot(latent_rows[:, :, key_rank:].reshape(-1, key_rank), uppers[1], pr...  12.1 us
    dot_general x4, matrix products, attend(): jnp.einsum('bgrln,bngd->blgrd', expo.astype(jnp.bfloat16), values_grp, pr...  11.4 us
    another operation x4, local copies, waits for them, and re-layouts  9.08 us
    dot_general x1, matrix products, body(): jnp.dot(flat_hidden, lax.all_gather(down_weight, 'dp', axis=0, tiled=True...  7.07 us
  transfers between devices with their start and end apart: 3, of which 3 were waited for; matrix products, arithmetic and copies ran while one was open for 4% of the time, Pallas kernels for 0%

commit v1 on v0

v1 whole, which is shorter than its diff:
```python
import functools
import math

import jax
import jax.numpy as jnp
import numpy as np
from jax import lax
from jax.experimental import pallas as pl
from jax.experimental.pallas import tpu as pltpu
from jax.sharding import PartitionSpec as P

HEAD = 128
WINDOW = 4096
MESH = pl.DeviceIdType.MESH

query_scale = 144.0 ** (-0.5)
soft_cap = 50.0
EXP_SCALE = soft_cap * math.log2(math.e)


def angle_tables(rows, blocks):
    half = HEAD // 2
    freqs = 10000.0 ** (-2.0 * np.arange(half, dtype=np.float64) / HEAD)
    freqs = np.concatenate([freqs, freqs])[None, :]
    sign = np.concatenate([-np.ones(half), np.ones(half)])[None, :]
    near = np.arange(rows, dtype=np.float64)[:, None] * freqs
    far = (rows * np.arange(blocks, dtype=np.float64))[:, None] * freqs
    near = np.stack([np.cos(near), sign * np.sin(near)]).astype(np.float32)
    far = np.stack([np.cos(far), sign * np.sin(far)]).astype(np.float32)
    return near, far


def piece_count(half):
    for pieces in (6, 5, 4, 3, 2):
        if half % (pieces * 16) == 0:
            return pieces
    return 1


def kernel(
    ring, pieces, lengths_ref, hidden_ref, q_ref, down_ref, up_ref, near_ref, far_ref,
    latent_out, attended_out,
    hid, q_raw, qs, wf, up, lat, acc, keys, values, numer, denom, out_buf,
    local_sem, x_send, x_recv, y_send, y_recv, c_send, c_recv, own_send, own_recv,
    up_send, up_recv, chain_send, pair_send, lat_recv, out_sem,
):
    seq = lax.axis_index("seq")
    dp = lax.axis_index("dp")
    rows = lat.shape[1]
    shard = down_ref.shape[0]
    half = shard // 2
    piece = half // pieces
    up_rows = up_ref.shape[1]
    groups = qs.shape[0]
    ratio = qs.shape[1] // rows
    key_rank = lat.shape[2] // 2
    total = ring * rows

    side = lax.rem(seq, 2)
    pair = seq + 1 - 2 * side
    core = lax.rem(dp, 2)
    mate = dp + 1 - 2 * core
    across = lax.rem(dp + 2, 4)
    diagonal = lax.rem(mate + 2, 4)
    has_next = seq + 2 < ring
    has_prev = seq >= 2

    def local(src, dst, sem):
        return pltpu.make_async_copy(src, dst, sem)

    loads = [
        local(down_ref, wf.at[dp], local_sem.at[0]),
        local(hidden_ref.at[0], hid, local_sem.at[1]),
        local(up_ref, up.at[:, pl.ds(pl.multiple_of(dp * up_rows, up_rows), up_rows), :], local_sem.at[2]),
        local(q_ref.at[0], q_raw, local_sem.at[3]),
    ]
    for load in loads:
        load.start()

    barrier = pltpu.get_barrier_semaphore()

    def greet(device):
        pl.semaphore_signal(barrier, inc=1, device_id=device, device_id_type=MESH)

    greet({"seq": seq, "dp": mate})
    greet({"seq": seq, "dp": across})
    greet({"seq": pair, "dp": dp})

    @pl.when(has_next)
    def _():
        greet({"seq": seq + 2, "dp": dp})

    @pl.when(has_prev)
    def _():
        greet({"seq": seq - 2, "dp": dp})

    pl.semaphore_wait(barrier, 3 + has_next.astype(jnp.int32) + has_prev.astype(jnp.int32))

    def remote(src, dst, send, recv, device):
        return pltpu.make_async_remote_copy(
            src_ref=src, dst_ref=dst, send_sem=send, recv_sem=recv, device_id=device, device_id_type=MESH
        )

    to_mate = {"seq": seq, "dp": mate}
    to_across = {"seq": seq, "dp": across}
    to_pair = {"seq": pair, "dp": dp}
    to_next = {"seq": lax.rem(seq + 2, ring), "dp": dp}

    def part(which, index):
        return pl.ds(pl.multiple_of(which * half + index * piece, 16), piece)

    def x_copy(index):
        return remote(
            down_ref.at[part(side, index)], wf.at[dp, part(side, index)],
            x_send.at[index], x_recv.at[index], to_across,
        )

    def y_copy(index):
        view = wf.at[across, part(side, index)]
        return remote(view, view, y_send.at[index], y_recv.at[index], to_pair)

    def c_copy(slot, which, index):
        view = wf.at[across, part(which, index)]
        return remote(view, view, c_send.at[slot, index], c_recv.at[slot, index], to_mate)

    x_copies = [x_copy(i) for i in range(pieces)]
    for copy in x_copies:
        copy.start()
    own_copy = remote(down_ref, wf.at[dp], own_send, own_recv, to_mate)
    own_copy.start()

    def up_view(owner):
        return up.at[:, pl.ds(pl.multiple_of(owner * up_rows, up_rows), up_rows), :]

    up_across = remote(up_ref, up_view(dp), up_send.at[0], up_recv.at[0], to_across)
    up_across.start()
    up_mate = remote(up_ref, up_view(dp), up_send.at[1], up_recv.at[1], to_mate)
    up_mate.start()

    loads[3].wait()
    for g in range(groups):
        for r in range(ratio):
            column = (g * ratio + r) * HEAD
            qs[g, r * rows : (r + 1) * rows, :] = q_raw[:, column : column + HEAD]
    numer[...] = jnp.zeros_like(numer)
    denom[...] = jnp.zeros_like(denom)

    def project(owner):
        columns = pl.ds(pl.multiple_of(owner * shard, 128), shard)
        return jnp.dot(hid[:, columns], wf[owner], preferred_element_type=jnp.float32)

    loads[1].wait()
    loads[0].wait()
    acc[...] = project(dp)

    y_copies = [y_copy(i) for i in range(pieces)]
    near_copies = [c_copy(0, side, i) for i in range(pieces)]
    far_copies = [c_copy(1, 1 - side, i) for i in range(pieces)]
    for i in range(pieces):
        x_copies[i].wait_recv()
        y_copies[i].start()
        near_copies[i].start()
        if i >= 1:
            y_copies[i - 1].wait_recv()
            far_copies[i - 1].start()
        if i == pieces - 1:
            own_copy.wait_recv()
            acc[...] += project(mate)
    y_copies[pieces - 1].wait_recv()
    far_copies[pieces - 1].start()
    acc[...] += project(across)
    for i in range(pieces):
        near_copies[i].wait_recv()
        far_copies[i].wait_recv()
    live_count = lengths_ref[0] - seq * rows
    total_rows = acc[...] + project(diagonal)
    live = lax.broadcasted_iota(jnp.int32, total_rows.shape, 0) < live_count
    lat[seq] = jnp.where(live, total_rows, 0.0).astype(jnp.bfloat16)

    def chain(block):
        view = lat.at[block]
        return remote(view, view, chain_send.at[block], lat_recv.at[block], to_next)

    def swap(block):
        view = lat.at[block]
        return remote(view, view, pair_send.at[block], lat_recv.at[block], to_pair)

    @pl.when(has_next)
    def _():
        chain(seq).start()

    @pl.when(side == 0)
    def _():
        swap(seq).start()

    latent_copy = local(lat.at[seq], latent_out.at[0], out_sem.at[groups])
    latent_copy.start()

    up_mate.wait_recv()
    up_across.wait_recv()
    up_relay = remote(up_view(across), up_view(across), up_send.at[2], up_recv.at[2], to_mate)
    up_relay.start()
    loads[2].wait()
    up_relay.wait_recv()

    def attend(block, distance, masked):
        latent = lat[block]
        near_cos, near_sin = near_ref[0], near_ref[1]
        far_cos = far_ref[0, pl.ds(block, 1), :]
        far_sin = far_ref[1, pl.ds(block, 1), :]
        cosine = near_cos * far_cos - near_sin * far_sin
        sine = near_sin * far_cos + near_cos * far_sin
        keys_raw = jnp.dot(latent[:, :key_rank], up[0], preferred_element_type=jnp.float32)
        for g in range(groups):
            head = keys_raw[:, g * HEAD : (g + 1) * HEAD]
            turned = head * cosine + pltpu.roll(head, HEAD // 2, 1) * sine
            keys[g] = turned.astype(jnp.bfloat16)
        values_raw = jnp.dot(latent[:, key_rank:], up[1], preferred_element_type=jnp.float32)
        for g in range(groups):
            values[g] = values_raw[:, g * HEAD : (g + 1) * HEAD].astype(jnp.bfloat16)
        if masked:
            shape = (rows, rows)
            gap = (
                lax.broadcasted_iota(jnp.int32, shape, 0)
                - lax.broadcasted_iota(jnp.int32, shape, 1)
                + distance * rows
            )
            allowed = (gap >= 0) & (gap < WINDOW)
            allowed = jnp.concatenate([allowed.astype(jnp.float32)] * ratio, axis=0)
        for g in range(groups):
            raw = lax.dot_general(
                qs[g], keys[g], (((1,), (1,)), ((), ())), preferred_element_type=jnp.float32
            )
            expo = jnp.exp2(EXP_SCALE * jnp.tanh(raw * (query_scale / soft_cap)))
            if masked:
                expo = expo * allowed
            partial = expo[:, :HEAD]
            for column in range(HEAD, rows, HEAD):
                partial = partial + expo[:, column : column + HEAD]
            denom[g] += partial
            numer[g] += jnp.dot(expo.astype(jnp.bfloat16), values[g], preferred_element_type=jnp.float32)

    attend(seq, 0, True)

    def step(k, carry):
        block = seq - k
        odd = lax.rem(k, 2) == 1

        @pl.when(odd & (k + 1 <= seq))
        def _():
            arrived = block - 1
            chain(arrived).wait_recv()

            @pl.when(has_next)
            def _():
                chain(arrived).start()

            swap(arrived).start()

        @pl.when(odd)
        def _():
            swap(block).wait_recv()

        if total <= WINDOW:
            attend(block, k, False)
        else:
            edge = (k + 1) * rows > WINDOW

            @pl.when(jnp.logical_not(edge))
            def _():
                attend(block, k, False)

            @pl.when(edge & ((k - 1) * rows < WINDOW))
            def _():
                attend(block, k, True)

        return carry

    lax.fori_loop(1, seq + 1, step, 0)

    live_rows = lax.broadcasted_iota(jnp.int32, (rows, HEAD), 0) < live_count
    width = ratio * HEAD
    for g in range(groups):
        result = numer[g] / jnp.sum(denom[g], axis=1, keepdims=True)
        for r in range(ratio):
            column = g * width + r * HEAD
            piece_out = jnp.where(live_rows, result[r * rows : (r + 1) * rows], 0.0)
            out_buf[:, column : column + HEAD] = piece_out.astype(jnp.bfloat16)
        columns = pl.ds(g * width, width)
        local(out_buf.at[:, columns], attended_out.at[0, :, columns], out_sem.at[g]).start()

    def drain(k, carry):
        block = seq - 2 * k

        @pl.when(has_next)
        def _():
            chain(block).wait_send()

        @pl.when((k > 0) | (side == 0))
        def _():
            swap(block).wait_send()

        return carry

    lax.fori_loop(0, seq // 2 + 1, drain, 0)
    for copy in x_copies + y_copies + near_copies + far_copies + [own_copy, up_across, up_mate, up_relay]:
        copy.wait_send()
    latent_copy.wait()
    for g in range(groups):
        columns = pl.ds(g * width, width)
        local(out_buf.at[:, columns], attended_out.at[0, :, columns], out_sem.at[g]).wait()


def body(ring, dp_size, hidden, queries, down_weight, up_weight, lengths):
    _, rows, model_dim = hidden.shape
    shard, rank = down_weight.shape
    kv_width = up_weight.shape[2]
    groups = kv_width // HEAD
    q_width = queries.shape[2]
    ratio = q_width // kv_width
    near, far = angle_tables(rows, ring)
    pieces = piece_count(shard // 2)
    any_spec = pl.BlockSpec(memory_space=pl.ANY)
    vmem_spec = pl.BlockSpec(memory_space=pltpu.VMEM)
    f32, bf16, dma = jnp.float32, jnp.bfloat16, pltpu.SemaphoreType.DMA
    return pl.pallas_call(
        functools.partial(kernel, ring, pieces),
        out_shape=(
            jax.ShapeDtypeStruct((1, rows, rank), bf16),
            jax.ShapeDtypeStruct((1, rows, q_width), bf16),
        ),
        in_specs=[pl.BlockSpec(memory_space=pltpu.SMEM)] + [any_spec] * 4 + [vmem_spec] * 2,
        out_specs=(any_spec, any_spec),
        scratch_shapes=[
            pltpu.VMEM((rows, model_dim), bf16),
            pltpu.VMEM((rows, q_width), bf16),
            pltpu.VMEM((groups, ratio * rows, HEAD), bf16),
            pltpu.VMEM((dp_size, shard, rank), bf16),
            pltpu.VMEM((2, dp_size * up_weight.shape[1], kv_width), bf16),
            pltpu.VMEM((ring, rows, rank), bf16),
            pltpu.VMEM((rows, rank), f32),
            pltpu.VMEM((groups, rows, HEAD), bf16),
            pltpu.VMEM((groups, rows, HEAD), bf16),
            pltpu.VMEM((groups, ratio * rows, HEAD), f32),
            pltpu.VMEM((groups, ratio * rows, HEAD), f32),
            pltpu.VMEM((rows, q_width), bf16),
            dma((4,)),
            dma((pieces,)), dma((pieces,)),
            dma((pieces,)), dma((pieces,)),
            dma((2, pieces)), dma((2, pieces)),
            dma, dma,
            dma((3,)), dma((3,)),
            dma((ring,)), dma((ring,)), dma((ring,)),
            dma((groups + 1,)),
        ],
        compiler_params=pltpu.CompilerParams(
            collective_id=0, has_side_effects=True, vmem_limit_bytes=60 * 1024 * 1024
        ),
    )(lengths, hidden, queries, down_weight, up_weight, jnp.asarray(near), jnp.asarray(far))


def solution(mesh):
    in_specs = (
        P("dp", "seq", None),
        P("dp", "seq", None),
        P("dp", None),
        P(None, "dp", None),
        P("dp"),
    )
    out_specs = (P("dp", "seq", None), P("dp", "seq", None))
    step = functools.partial(body, mesh.shape["seq"], mesh.shape["dp"])
    return jax.shard_map(step, mesh=mesh, in_specs=in_specs, out_specs=out_specs, check_vma=False)
```

time: 271 us -> 101 us (0.37); the launches traced: 266 us -> 101 us
  waiting for transfers between devices: 152 us -> 0 us
  Pallas kernels: 0 us -> 95.4 us
  matrix products: 47.4 us -> 0 us
  local copies, waits for them, and re-layouts: 33.7 us -> 4.17 us
  other arithmetic: 14.5 us -> 0 us
  between operations: 14.5 us -> 1.29 us
  loops' own time: 3.1 us -> 0 us
    all_gather x3 -> x0, waiting for transfers between devices: 152 us -> none  [the longest x1 73.1 us: body(): part = lax.all_gather(latent, 'seq', axis=1, tiled=True)]
    pallas_call x0 -> x1, Pallas kernels: none -> 95.4 us  [body(): pl.pallas_call(functools.partial(kernel, ring, pieces), out_shape=(jax.Sh...]
    dot_general x17 -> x0, matrix products: 47.4 us -> none  [the longest x4 13.8 us: attend(): jnp.einsum('blgrd,bngd->bgrln', q_split, keys_grp, preferred_element_type...]
    another operation x4 -> x0, local copies, waits for them, and re-layouts: 9.08 us -> none
    while x64 -> x0, local copies, waits for them, and re-layouts: 5.45 us -> none
    slice x4 -> x0, local copies, waits for them, and re-layouts: 5.31 us -> none  [expand(): uppers[0]]
    squeeze x4 -> x0, local copies, waits for them, and re-layouts: 5.17 us -> none  [body(): lax.scan(scan_step, initial, (jnp.arange(pieces, dtype=jnp.int32), shaped))]
    cos x4 -> x0, other arithmetic: 4.76 us -> none  [rotate(): cosine = jnp.cos(angles)[None, :, None, :]]
  transfers between devices with their start and end apart: 3 -> 0, of which waited for: 3 -> 0; matrix products, arithmetic and copies ran while one was open for 4% -> 0% of each run, Pallas kernels for 0% -> 0%
where the time goes in v1:
time: 101 us
  Pallas kernels  95.4 us (94%)
  local copies, waits for them, and re-layouts  4.17 us (4%)
  between operations  1.29 us (1%)
    pallas_call x1, Pallas kernels, body(): pl.pallas_call(functools.partial(kernel, ring, pieces), out_shape=(jax.Sh...  95.4 us
    unnamed x2, local copies, waits for them, and re-layouts  4.17 us

profile of v1, /device:TPU:28, one launch (start us, length us, event | category | flops | bytes accessed | tf_op | source)
XLA Modules:
  0.0 100.8 jit_solution(16660300733374209377)
XLA Ops:
  1.3 95.4 %shard_map.86 = (bf16[1,256,1024]{2,1,0:T(8,128)(2,1)}, bf16[1,256,2048]{2,1,0:T(8,128)(2,1)}) custom-call(s32[1]{0:T(128)S(6)} %copy.11.lengths_ref, bf16[1,256,4608]{2,1,0:T(8,128)(2,1)} %hidden_ref.1, bf16[1,256,2048]{2,1,0:T(8,128)(2,1)} %q_ref.1, bf16[1152,1024]{1,0:T(8,128)(2,1)} %down_ref.1, bf16[2,128,1024]{2,1,0:T(8,128)(2,1)} %up_ref.1, ...), custom_call_target="tpu_custom_call" | custom-call | tf_op jit(solution)/shard_map/pallas_call | solution.py:326
  96.7 1.9 %copy.12 = bf16[1,256,1024]{2,1,0:T(8,128)(2,1)} copy(bf16[1,256,1024]{2,1,0:T(8,128)(2,1)} %get-tuple-element.4) | data formatting | bytes 1048576
  98.5 2.3 %copy.13 = bf16[1,256,2048]{2,1,0:T(8,128)(2,1)} copy(bf16[1,256,2048]{2,1,0:T(8,128)(2,1)} %get-tuple-element.5) | data formatting | bytes 2097152

commit v2 on v1

--- a/solution.py
+++ b/solution.py
@@ -30,26 +30,28 @@
     return near, far
 
 
-def piece_count(half):
-    for pieces in (6, 5, 4, 3, 2):
-        if half % (pieces * 16) == 0:
+def piece_count(quarter):
+    for pieces in (6, 4, 2):
+        if quarter % (pieces * 16) == 0:
             return pieces
-    return 1
+    return 2
 
 
 def kernel(
     ring, pieces, lengths_ref, hidden_ref, q_ref, down_ref, up_ref, near_ref, far_ref,
     latent_out, attended_out,
     hid, q_raw, qs, wf, up, lat, acc, keys, values, numer, denom, out_buf,
-    local_sem, x_send, x_recv, y_send, y_recv, c_send, c_recv, own_send, own_recv,
+    local_sem, x_send, x_recv, y_send, y_recv, z_send, z_recv, c_send, c_recv, own_send, own_recv,
     up_send, up_recv, chain_send, pair_send, lat_recv, out_sem,
 ):
     seq = lax.axis_index("seq")
     dp = lax.axis_index("dp")
     rows = lat.shape[1]
     shard = down_ref.shape[0]
-    half = shard // 2
-    piece = half // pieces
+    quarter = shard // 4
+    piece = quarter // pieces
+    split = pieces // 2
+    half_rows = rows // 2
     up_rows = up_ref.shape[1]
     groups = qs.shape[0]
     ratio = qs.shape[1] // rows
@@ -58,6 +60,12 @@
 
     side = lax.rem(seq, 2)
     pair = seq + 1 - 2 * side
+    level = lax.rem(seq // 2, 2)
+    fellow = seq + 2 - 4 * level
+    own_part = 2 * side + level
+    pair_part = 2 - 2 * side + level
+    fellow_part = 2 * side + 1 - level
+    diagonal_part = 3 - own_part
     core = lax.rem(dp, 2)
     mate = dp + 1 - 2 * core
     across = lax.rem(dp + 2, 4)
@@ -104,20 +112,25 @@
     to_mate = {"seq": seq, "dp": mate}
     to_across = {"seq": seq, "dp": across}
     to_pair = {"seq": pair, "dp": dp}
+    to_fellow = {"seq": fellow, "dp": dp}
     to_next = {"seq": lax.rem(seq + 2, ring), "dp": dp}
 
     def part(which, index):
-        return pl.ds(pl.multiple_of(which * half + index * piece, 16), piece)
+        return pl.ds(pl.multiple_of(which * quarter + index * piece, 16), piece)
 
     def x_copy(index):
         return remote(
-            down_ref.at[part(side, index)], wf.at[dp, part(side, index)],
+            down_ref.at[part(own_part, index)], wf.at[dp, part(own_part, index)],
             x_send.at[index], x_recv.at[index], to_across,
         )
 
-    def y_copy(index):
-        view = wf.at[across, part(side, index)]
-        return remote(view, view, y_send.at[index], y_recv.at[index], to_pair)
+    def y_copy(which, slot):
+        view = wf.at[across, part(which, slot % pieces)]
+        return remote(view, view, y_send.at[slot], y_recv.at[slot], to_pair)
+
+    def z_copy(which, slot):
+        view = wf.at[across, part(which, slot % pieces)]
+        return remote(view, view, z_send.at[slot], z_recv.at[slot], to_fellow)
 
     def c_copy(slot, which, index):
         view = wf.at[across, part(which, index)]
@@ -153,45 +166,70 @@
     loads[0].wait()
     acc[...] = project(dp)
 
-    y_copies = [y_copy(i) for i in range(pieces)]
-    near_copies = [c_copy(0, side, i) for i in range(pieces)]
-    far_copies = [c_copy(1, 1 - side, i) for i in range(pieces)]
+    y_copies = [y_copy(own_part, i) for i in range(pieces)]
+    z_copies = [z_copy(own_part, i) for i in range(pieces)]
+    relays = [
+        y_copy(fellow_part, pieces + i) if i < split else z_copy(pair_part, pieces + i)
+        for i in range(pieces)
+    ]
+    mate_copies = [
+        [c_copy(slot, which, i) for i in range(pieces)]
+        for slot, which in enumerate((own_part, pair_part, fellow_part, diagonal_part))
+    ]
+
+    def pass_on(i):
+        y_copies[i].wait_recv()
+        if i >= split:
+            relays[i].start()
+        mate_copies[1][i].start()
+        z_copies[i].wait_recv()
+        if i < split:
+            relays[i].start()
+        mate_copies[2][i].start()
+
     for i in range(pieces):
         x_copies[i].wait_recv()
         y_copies[i].start()
-        near_copies[i].start()
+        z_copies[i].start()
+        mate_copies[0][i].start()
         if i >= 1:
-            y_copies[i - 1].wait_recv()
-            far_copies[i - 1].start()
-        if i == pieces - 1:
-            own_copy.wait_recv()
-            acc[...] += project(mate)
-    y_copies[pieces - 1].wait_recv()
-    far_copies[pieces - 1].start()
+            pass_on(i - 1)
+    pass_on(pieces - 1)
+    own_copy.wait_recv()
+    acc[...] += project(mate)
+    for i in range(pieces):
+        relays[i].wait_recv()
+        mate_copies[3][i].start()
     acc[...] += project(across)
-    for i in range(pieces):
-        near_copies[i].wait_recv()
-        far_copies[i].wait_recv()
+    for copies in mate_copies:
+        for copy in copies:
+            copy.wait_recv()
     live_count = lengths_ref[0] - seq * rows
     total_rows = acc[...] + project(diagonal)
     live = lax.broadcasted_iota(jnp.int32, total_rows.shape, 0) < live_count
     lat[seq] = jnp.where(live, total_rows, 0.0).astype(jnp.bfloat16)
 
-    def chain(block):
-        view = lat.at[block]
-        return remote(view, view, chain_send.at[block], lat_recv.at[block], to_next)
-
-    def swap(block):
-        view = lat.at[block]
-        return remote(view, view, pair_send.at[block], lat_recv.at[block], to_pair)
+    def chain(block, part_index):
+        view = lat.at[block, pl.ds(part_index * half_rows, half_rows)]
+        return remote(
+            view, view, chain_send.at[block, part_index], lat_recv.at[block, part_index], to_next
+        )
+
+    def swap(block, part_index):
+        view = lat.at[block, pl.ds(part_index * half_rows, half_rows)]
+        return remote(
+            view, view, pair_send.at[block, part_index], lat_recv.at[block, part_index], to_pair
+        )
 
     @pl.when(has_next)
     def _():
-        chain(seq).start()
+        chain(seq, 0).start()
+        chain(seq, 1).start()
 
     @pl.when(side == 0)
     def _():
-        swap(seq).start()
+        swap(seq, 0).start()
+        swap(seq, 1).start()
 
     latent_copy = local(lat.at[seq], latent_out.at[0], out_sem.at[groups])
     latent_copy.start()
@@ -249,17 +287,29 @@
         @pl.when(odd & (k + 1 <= seq))
         def _():
             arrived = block - 1
-            chain(arrived).wait_recv()
-
-            @pl.when(has_next)
-            def _():
-                chain(arrived).start()
-
-            swap(arrived).start()
+            for h in range(2):
+                chain(arrived, h).wait_recv()
+
+                @pl.when(has_next)
+                def _():
+                    chain(arrived, h).start()
+
+                if h == 0:
+                    swap(arrived, h).start()
+                else:
+
+                    @pl.when(arrived > 0)
+                    def _():
+                        swap(arrived, h).start()
 
         @pl.when(odd)
         def _():
-            swap(block).wait_recv()
+            swap(block, 0).wait_recv()
+            swap(block, 1).wait_recv()
+
+            @pl.when((block == 0) & has_next & (side == 1))
+            def _():
+                chain(block, 1).start()
 
         if total <= WINDOW:
             attend(block, k, False)
@@ -294,16 +344,26 @@
 
         @pl.when(has_next)
         def _():
-            chain(block).wait_send()
+            chain(block, 0).wait_send()
+            chain(block, 1).wait_send()
 
         @pl.when((k > 0) | (side == 0))
         def _():
-            swap(block).wait_send()
+            swap(block, 0).wait_send()
+
+        @pl.when((side == 1) & (k > 0) | (side == 0) & ((block > 0) | (seq == 0)))
+        def _():
+            swap(block, 1).wait_send()
 
         return carry
 
     lax.fori_loop(0, seq // 2 + 1, drain, 0)
-    for copy in x_copies + y_copies + near_copies + far_copies + [own_copy, up_across, up_mate, up_relay]:
+
+    @pl.when(has_next & (side == 1))
+    def _():
+        chain(0, 1).wait_send()
+
+    for copy in x_copies + y_copies + z_copies + relays + sum(mate_copies, []) + [own_copy, up_across, up_mate, up_relay]:
         copy.wait_send()
     latent_copy.wait()
     for g in range(groups):
@@ -319,7 +379,7 @@
     q_width = queries.shape[2]
     ratio = q_width // kv_width
     near, far = angle_tables(rows, ring)
-    pieces = piece_count(shard // 2)
+    pieces = piece_count(shard // 4)
     any_spec = pl.BlockSpec(memory_space=pl.ANY)
     vmem_spec = pl.BlockSpec(memory_space=pltpu.VMEM)
     f32, bf16, dma = jnp.float32, jnp.bfloat16, pltpu.SemaphoreType.DMA
@@ -346,11 +406,12 @@
             pltpu.VMEM((rows, q_width), bf16),
             dma((4,)),
             dma((pieces,)), dma((pieces,)),
-            dma((pieces,)), dma((pieces,)),
-            dma((2, pieces)), dma((2, pieces)),
+            dma((2 * pieces,)), dma((2 * pieces,)),
+            dma((2 * pieces,)), dma((2 * pieces,)),
+            dma((4, pieces)), dma((4, pieces)),
             dma, dma,
             dma((3,)), dma((3,)),
-            dma((ring,)), dma((ring,)), dma((ring,)),
+            dma((ring, 2)), dma((ring, 2)), dma((ring, 2)),
             dma((groups + 1,)),
         ],
         compiler_params=pltpu.CompilerParams(

time: 101 us -> 89.6 us (0.89)
  the two profiles are of different devices: /device:TPU:28 before, /device:TPU:24 now
where the time goes in v2:
time: 89.6 us; the launch traced here: 89.3 us
  Pallas kernels  83.9 us (94%)
  local copies, waits for them, and re-layouts  4.17 us (5%)
  between operations  1.29 us (1%)
    pallas_call x1, Pallas kernels, body(): pl.pallas_call(functools.partial(kernel, ring, pieces), out_shape=(jax.Sh...  83.9 us
    unnamed x2, local copies, waits for them, and re-layouts  4.17 us

profile of v2, /device:TPU:24, one launch (start us, length us, event | category | flops | bytes accessed | tf_op | source)
XLA Modules:
  0.0 89.3 jit_solution(16270367250245928945)
XLA Ops:
  1.3 83.9 %shard_map.86 = (bf16[1,256,1024]{2,1,0:T(8,128)(2,1)}, bf16[1,256,2048]{2,1,0:T(8,128)(2,1)}) custom-call(s32[1]{0:T(128)S(6)} %copy.11.lengths_ref, bf16[1,256,4608]{2,1,0:T(8,128)(2,1)} %hidden_ref.1, bf16[1,256,2048]{2,1,0:T(8,128)(2,1)} %q_ref.1, bf16[1152,1024]{1,0:T(8,128)(2,1)} %down_ref.1, bf16[2,128,1024]{2,1,0:T(8,128)(2,1)} %up_ref.1, ...), custom_call_target="tpu_custom_call" | custom-call | tf_op jit(solution)/shard_map/pallas_call | solution.py:386
  85.2 1.9 %copy.12 = bf16[1,256,1024]{2,1,0:T(8,128)(2,1)} copy(bf16[1,256,1024]{2,1,0:T(8,128)(2,1)} %get-tuple-element.4) | data formatting | bytes 1048576
  87.0 2.3 %copy.13 = bf16[1,256,2048]{2,1,0:T(8,128)(2,1)} copy(bf16[1,256,2048]{2,1,0:T(8,128)(2,1)} %get-tuple-element.5) | data formatting | bytes 2097152
